TPU v7x, 32 devices: a whole 2x2x4 slice. The times are simulated.
32 devices in a mesh: views: 8 (over z, y), rows: 4 (over x, core).
Axes of the slice: x: 2, y: 2, z: 4, core: 2. Of those that a mesh axis runs over, the one named last changes fastest.
Arguments:
- sinogram: bfloat16 [8, 64, 2048], P(None, 'views'), may hold values from -32 to 6176
- view_shift: int32 [64], P('views'), may hold values from -48 to 48
- conv_one: float32 [9, 32], replicated, may hold values from -2 to 2
- bias_one: float32 [32], replicated, may hold values from -3 to 3
- conv_two: bfloat16 [32, 288], replicated, may hold values from -0.375 to 0.375
- bias_two: float32 [32], replicated, may hold values from -3 to 3
Outputs:
- denoised: bfloat16 [8, 32, 16, 2048], P('views', None, 'rows')
All inputs are finite; a program needn't handle non-finite values.
Results may differ from a plain program's by a relative error of at most 0.008.
Values may be sent and summed in bfloat16 or wider, within the bound.
A program may use at most 64 MiB of HBM per device.

v0:
```python
import math

import jax
import jax.numpy as jnp
from jax import lax
from jax.sharding import PartitionSpec as P

BINS = 2048
WIDTH = 2048
TILE = 256
MARGIN = 384
ROW_DEV = 4


def extended_2(cells, sides, width):
    for axis, dim in sides:
        count = lax.axis_size(axis)
        ends = count - 1
        head = lax.slice_in_dim(cells, 0, width, axis=dim)
        tail = lax.slice_in_dim(cells, cells.shape[dim] - width, cells.shape[dim], axis=dim)
        cells = jnp.concatenate(
            [
                lax.ppermute(tail, axis, [(i, (i + 1) % count) for i in range(ends)]),
                cells,
                lax.ppermute(head, axis, [((i + 1) % count, i) for i in range(ends)]),
            ],
            axis=dim,
        )
    return cells


def ramp_table(detector):
    indices = jnp.arange(detector, dtype=jnp.int32)
    offset = indices[None, :] - indices[:, None]
    square = (offset * offset).astype(jnp.float32)
    guarded = jnp.maximum(square, 1.0)
    is_odd = offset % 2 != 0
    values = jnp.where(
        offset == 0, 0.25, jnp.where(is_odd, -1.0 / (math.pi * math.pi * guarded), 0.0)
    )
    return values


def filter_views(sinogram):
    sheets, view_count, detector = sinogram.shape
    table = ramp_table(detector)
    flat = sinogram.reshape(sheets * view_count, detector).astype(jnp.float32)
    result = jnp.dot(
        flat, table, precision=lax.Precision.HIGHEST, preferred_element_type=jnp.float32
    )
    return result.astype(jnp.bfloat16).reshape(sheets, view_count, detector)


def backproject(padded, view_shift, first_view, row_base, row_count, image_rows, views_total):
    sheets, view_count, extended_bins = padded.shape
    tiles = WIDTH // TILE
    band_bins = min(TILE + 128, extended_bins)
    columns = (jnp.arange(WIDTH, dtype=jnp.float32) - (WIDTH - 1) / 2.0).reshape(tiles, TILE)
    rows_y = (row_base + jnp.arange(row_count, dtype=jnp.int32)).astype(jnp.float32) - (
        image_rows - 1
    ) / 2.0
    band_offsets = jnp.arange(band_bins, dtype=jnp.int32)

    def one_view(view, running):
        sheet = lax.dynamic_index_in_dim(padded, view, 1, keepdims=False)
        shift = lax.dynamic_index_in_dim(view_shift, view, 0, keepdims=False)
        angle = (first_view + view).astype(jnp.float32) * (math.pi / views_total)
        cosine = jnp.cos(angle)
        sine = jnp.sin(angle)
        center = shift.astype(jnp.float32) + ((BINS - 1) / 2.0 + MARGIN)
        pieces = []
        for tile_index in range(tiles):
            position = columns[tile_index][None, :] * cosine + rows_y[:, None] * sine + center
            lowest = jnp.min(position)
            band_start = jnp.clip(
                jnp.floor(lowest).astype(jnp.int32) - 1, 0, extended_bins - band_bins
            )
            band = lax.dynamic_slice_in_dim(sheet, band_start, band_bins, 1)
            bin_place = (band_start + band_offsets).astype(jnp.float32)
            weights = jnp.maximum(
                0.0, 1.0 - jnp.abs(position[:, :, None] - bin_place[None, None, :])
            )
            weights = weights.astype(jnp.bfloat16)
            pieces.append(
                jnp.einsum("rtb,sb->srt", weights, band, preferred_element_type=jnp.float32)
            )
        return running + jnp.concatenate(pieces, axis=2)

    start = jnp.zeros((sheets, row_count, WIDTH), jnp.float32)
    return lax.fori_loop(0, view_count, one_view, start)


def first_layer(extended, conv_one, bias_one):
    row_count = extended.shape[1] - 2
    columns = extended.shape[2]
    padded = jnp.pad(extended.astype(jnp.float32), ((0, 0), (0, 0), (1, 1)))
    running = jnp.zeros((extended.shape[0], conv_one.shape[1], row_count, columns), jnp.float32)
    running = running + bias_one[None, :, None, None]
    for kernel_tap in range(9):
        row_off = kernel_tap // 3
        col_off = kernel_tap % 3
        window = padded[:, row_off : row_off + row_count, col_off : col_off + columns]
        running = running + conv_one[kernel_tap][None, :, None, None] * window[:, None]
    return jnp.maximum(running, 0.0).astype(jnp.bfloat16)


def second_layer(extended, conv_two, bias_two):
    sheets, channels, rows_ext, columns = extended.shape
    row_count = rows_ext - 2
    padded = jnp.pad(extended, ((0, 0), (0, 0), (0, 0), (1, 1)))
    windows = [
        padded[
            :,
            :,
            kernel_tap // 3 : kernel_tap // 3 + row_count,
            kernel_tap % 3 : kernel_tap % 3 + columns,
        ]
        for kernel_tap in range(9)
    ]
    stacked = jnp.stack(windows, axis=1).reshape(sheets, 9 * channels, row_count * columns)
    mixed = jnp.einsum("ok,skn->son", conv_two, stacked, preferred_element_type=jnp.float32)
    mixed = mixed + bias_two[None, :, None]
    return (
        jnp.maximum(mixed, 0.0).astype(jnp.bfloat16).reshape(sheets, channels, row_count, columns)
    )


def local(sinogram, view_shift, conv_one, bias_one, conv_two, bias_two):
    sheets, view_count, detector = sinogram.shape
    row_groups = lax.axis_size("rows")
    views_total = view_count * lax.axis_size("views")
    image_rows = ROW_DEV * row_groups
    filtered = filter_views(sinogram)
    padded = jnp.pad(filtered, ((0, 0), (0, 0), (MARGIN, MARGIN)))
    first_view = lax.axis_index("views") * view_count
    row_base = lax.axis_index("rows") * ROW_DEV
    partial_term = backproject(
        padded, view_shift, first_view, row_base, ROW_DEV, image_rows, views_total
    )
    summed = lax.psum_scatter(partial_term, "views", scatter_dimension=0, tiled=True)
    image = (summed * (math.pi / views_total)).astype(jnp.bfloat16)
    extended = extended_2(image, (("rows", 1),), 2)
    hidden = first_layer(extended, conv_one, bias_one)
    global_rows = row_base - 1 + jnp.arange(ROW_DEV + 2, dtype=jnp.int32)
    inside = (global_rows >= 0) & (global_rows < image_rows)
    hidden_ext = jnp.where(inside[None, None, :, None], hidden, jnp.zeros_like(hidden))
    return second_layer(hidden_ext, conv_two, bias_two)


def solution(mesh):
    return jax.shard_map(
        local,
        mesh=mesh,
        in_specs=(P(None, "views", None), P("views"), P(), P(), P(), P()),
        out_specs=P("views", None, "rows", None),
        check_vma=False,
    )
```

profile of v0, /device:TPU:1, one launch (start us, length us, event | category | flops | bytes accessed | tf_op | source)
XLA Modules:
  0.0 218.9 jit_solution(4353812493349233005)
XLA Ops:
  6.6 0.9 copy-done
  7.5 19.6 %fusion.115 = bf16[8,8,2048]{2,1,0:T(8,128)(2,1)S(1)} fusion(bf16[8,8,2048]{2,1,0:T(8,128)(2,1)S(1)} %copy-done), kind=kOutput, calls=%fused_computation.156 | convolution fusion | flops 3309436928 | bytes 524288 | tf_op jit(solution)/shard_map/dot_general | solution.py:48
  27.4 86.1 %while.18 = (s32[]{:T(128)}, f32[8,4,2048]{2,0,1:T(8,128)S(1)}, f32[8,256]{1,0:T(8,128)S(1)}, s32[]{:T(128)}, s32[8]{0:T(128)S(1)}, /*index=5*/bf16[8,8,2816]{2,...) while((s32[]{:T(128)}, f32[8,4,2048]{2,0,1:T(8,128)S(1)}, ...), condition=%wide.region_9.10_spmd.clone.clone, body=%wide.region_0.9_spmd.clone.clone.sunk | while | flops 66224160 | bytes 1217479 | solution.py:90
  28.7 0.8 fusion.172
  39.5 0.8 fusion.172
  50.3 0.8 fusion.172
  61.0 0.8 fusion.172
  71.8 0.8 fusion.172
  82.5 0.8 fusion.172
  93.3 0.8 fusion.172
  104.0 0.8 fusion.172
  113.5 0.9 copy.9
  115.0 70.7 %all-reduce.6.cloned.1.call-done = f32[8,4,2048]{2,1,0:T(4,128)} async-done(((f32[8,4,2048]{2,1,0:T(4,128)}), f32[8,4,2048]{2,1,0:T(4,128)}) %all-reduce.6.cloned.1.call-update) | async-done | bytes 262160
  185.7 1.4 fusion.135
  187.1 5.5 %collective-permute-start = (bf16[1,2,2048]{2,1,0:T(2,128)(2,1)S(1)}, bf16[1,2,2048]{2,1,0:T(2,128)(2,1)S(1)}, u32[]{:S(2)}, u32[]{:S(2)}) collective-permute-start(bf16[1,2,2048]{2,1,0:T(2,128)(2,1)S(1)} %get-tuple-element.405), channel_id=1, source_target_pairs={{0,1},{1,2},{2,3},{4,5},{5,6},{6,7},{8,9},{9,10},{10,11},{12,13},{... | collective-permute-start | bytes 24584 | tf_op jit(solution)/shard_map/ppermute | solution.py:23
  192.7 1.9 collective-permute-start.1
  194.6 3.0 %collective-permute-done.1 = bf16[1,2,2048]{2,1,0:T(2,128)(2,1)S(1)} collective-permute-done((bf16[1,2,2048]{2,1,0:T(2,128)(2,1)S(1)}, bf16[1,2,2048]{2,1,0:T(2,128)(2,1)S(1)}, u32[]{:S(2)}, u32[]{:S(2)}) %collective-permute-start.1) | collective-permute-done | bytes 8224 | tf_op jit(solution)/shard_map/ppermute | solution.py:25
  197.8 2.0 fusion.118
  201.0 0.7 fusion.124
  202.0 0.7 fusion.126
  202.7 0.7 fusion.128
  204.4 5.4 %copy.10 = bf16[36,8,4,2048]{3,1,2,0:T(8,128)(2,1)S(1)} copy(bf16[36,8,4,2048]{3,2,1,0:T(4,128)(2,1)S(1)} %bitcast.173) | data formatting | bytes 9437184
  209.9 1.0 fusion.103
  210.9 1.2 reshape.631
  (192 shorter events, 36.4 us)
Async XLA Ops:
  6.5 1.0 copy-start
  6.5 179.2 %all-reduce.6.cloned.1.call-start = ((), (), s32[]{:S(2)}) async-start(), calls=%async_computation | async-start | bytes 524288
  7.5 19.8 %copy-start.5 = (s32[8]{0:T(128)S(1)}, s32[8]{0:T(128)}, u32[]{:S(2)}) copy-start(s32[8]{0:T(128)} %param.9) | copy-start | bytes 100
  27.3 87.0 %copy-start.6 = (u32[32]{0:T(128)S(1)}, u32[32]{0:T(128)}, u32[]{:S(2)}) copy-start(u32[32]{0:T(128)} %constant.611) | copy-start | bytes 388
  27.4 87.7 %copy-start.2 = (f32[9,32]{1,0:T(8,128)S(1)}, f32[9,32]{1,0:T(8,128)}, u32[]{:S(2)}) copy-start(f32[9,32]{1,0:T(8,128)} %param.10) | copy-start | bytes 3460
  27.4 170.5 %copy-start.3 = (f32[32]{0:T(128)S(1)}, f32[32]{0:T(128)}, u32[]{:S(2)}) copy-start(f32[32]{0:T(128)} %param.11) | copy-start | bytes 388
  187.1 7.5 %collective-permute-start = (bf16[1,2,2048]{2,1,0:T(2,128)(2,1)S(1)}, bf16[1,2,2048]{2,1,0:T(2,128)(2,1)S(1)}, u32[]{:S(2)}, u32[]{:S(2)}) collective-permute-start(bf16[1,2,2048]{2,1,0:T(2,128)(2,1)S(1)} %get-tuple-element.405), channel_id=1, source_target_pairs={{0,1},{1,2},{2,3},{4,5},{5,6},{6,7},{8,9},{9,10},{10,11},{12,13},{... | collective-permute-start | bytes 24584 | tf_op jit(solution)/shard_map/ppermute | solution.py:23
  192.7 5.0 %collective-permute-start.1 = (bf16[1,2,2048]{2,1,0:T(2,128)(2,1)S(1)}, bf16[1,2,2048]{2,1,0:T(2,128)(2,1)S(1)}, u32[]{:S(2)}, u32[]{:S(2)}) collective-permute-start(bf16[1,2,2048]{2,1,0:T(2,128)(2,1)S(1)} %get-tuple-element.406), channel_id=1, source_target_pairs={{1,0},{2,1},{3,2},{5,4},{6,5},{7,6},{9,8},{10,9},{11,10},{13,12},{... | collective-permute-start | bytes 24584 | tf_op jit(solution)/shard_map/ppermute | solution.py:25
  204.4 5.4 %copy-start.1 = (bf16[32,288]{1,0:T(8,128)(2,1)S(1)}, bf16[32,288]{1,0:T(8,128)(2,1)}, u32[]{:S(2)}) copy-start(bf16[32,288]{1,0:T(8,128)(2,1)} %param.12) | copy-start | bytes 55300
  204.4 5.4 %copy-start.4 = (f32[32]{0:T(128)S(1)}, f32[32]{0:T(128)}, u32[]{:S(2)}) copy-start(f32[32]{0:T(128)} %param.13) | copy-start | bytes 388
Sparse Core Ops, SparseCore 0:
  114.5 71.2 all-reduce.5
where the time goes:
time: 220 us; the launch traced here: 219 us
  waiting for transfers between devices  73.7 us (34%)
  matrix products  47.7 us (22%)
  loops' own time  47 us (21%)
  local copies, waits for them, and re-layouts  18.6 us (8%)
  between operations  13.6 us (6%)
  other arithmetic  10.8 us (5%)
  starting transfers between devices  7.42 us (3%)
    unnamed x2, waiting for transfers between devices  70.7 us
    another operation x1, loops' own time, backproject(): return lax.fori_loop(0, view_count, one_view, start)  47 us
    dot_general x64, matrix products, one_view(): jnp.einsum('rtb,sb->srt', weights, band, preferred_element_type=jnp.float32)  27.1 us
    dot_general x1, matrix products, filter_views(): jnp.dot(flat, table, precision=lax.Precision.HIGHEST, preferred_element_t...  19.6 us
    unnamed x24, local copies, waits for them, and re-layouts  10.9 us
    reduce_min x8, other arithmetic, one_view(): lowest = jnp.min(position)  6.2 us
    ppermute x1, starting transfers between devices, extended_2(): lax.ppermute(tail, axis, [(i, (i + 1) % count) for i in range(ends)])  5.5 us
    dynamic_slice x8, local copies, waits for them, and re-layouts, one_view(): shift = lax.dynamic_index_in_dim(view_shift, view, 0, keepdims=False)  4.64 us
  transfers between devices with their start and end apart: 3, of which 2 were waited for; matrix products, arithmetic and copies ran while one was open for 0% of the time, Pallas kernels for 0%

commit v1 on v0

v1 whole, which is shorter than its diff:
```python
import functools
import math

import jax
import jax.numpy as jnp
import numpy as np
from jax import lax
from jax.experimental import pallas as pl
from jax.experimental.pallas import tpu as pltpu
from jax.sharding import PartitionSpec as P

MARGIN = 384
ROW_DEV = 4
LANES = 128
BLOCK = 256
QUARTERS = 4
F32 = jnp.float32
BF16 = jnp.bfloat16
MESH = pl.DeviceIdType.MESH


def split_parts(values, count):
    parts = []
    rest = values
    for part in range(count):
        piece = rest.astype(BF16)
        parts.append(piece)
        if part + 1 < count:
            rest = rest - piece.astype(F32)
    return parts


def ramp_block(block_offset):
    rows = lax.broadcasted_iota(jnp.int32, (BLOCK, BLOCK), 0)
    cols = lax.broadcasted_iota(jnp.int32, (BLOCK, BLOCK), 1)
    offset = cols - rows + block_offset * BLOCK
    square = (offset * offset).astype(F32)
    taps = jnp.where((offset & 1) != 0, (-1.0 / (math.pi * math.pi)) / jnp.maximum(square, 1.0), 0.0)
    if block_offset == 0:
        taps = jnp.where(offset == 0, 0.25, taps)
    return taps


def dot(a, b):
    return lax.dot_general(a, b, (((1,), (0,)), ((), ())), preferred_element_type=F32)


def dot_t(a, b):
    return lax.dot_general(a, b, (((1,), (1,)), ((), ())), preferred_element_type=F32)


def project_kernel(views_total, image_rows, sino_ref, perm_in_ref, perm_out_ref, shift_ref, cos_ref, sin_ref,
                   out_ref, sum_ref, low_ref, high_ref, part_ref):
    slices, view_count, bins = sino_ref.shape
    width = bins
    flat = slices * view_count
    blocks = bins // BLOCK
    ordered = dot(perm_in_ref[...], sino_ref[...].reshape(flat, bins)).astype(BF16)
    stacked = jnp.concatenate([ordered[:, k * BLOCK:(k + 1) * BLOCK] for k in range(blocks)], axis=0)
    for step in range(blocks):
        parts = split_parts(ramp_block(step), 3 if step < 2 else 2)
        count = (blocks - step) * flat
        down = stacked[:count]
        forward = sum(dot(down, part) for part in parts[::-1])
        if step == 0:
            sum_ref[...] = forward
        else:
            sum_ref[pl.ds(step * flat, count), :] += forward
            up = stacked[step * flat:]
            backward = sum(dot_t(up, part) for part in parts[::-1])
            sum_ref[pl.ds(0, count), :] += backward
    extended = low_ref.shape[1]
    low_ref[:, :MARGIN] = jnp.zeros((flat, MARGIN), F32)
    low_ref[:, MARGIN + bins:] = jnp.zeros((flat, extended - MARGIN - bins), F32)
    for k in range(blocks):
        low_ref[:, MARGIN + k * BLOCK:MARGIN + (k + 1) * BLOCK] = (
            sum_ref[k * flat:(k + 1) * flat, :].astype(BF16).astype(F32)
        )
    high_ref[...] = pltpu.roll(low_ref[...], extended - 1, 1)

    first_view = lax.axis_index("views") * view_count
    row_base = lax.axis_index("rows") * ROW_DEV
    half = (width - 1) / 2.0
    lanes = lax.broadcasted_iota(jnp.int32, (slices, LANES), 1).astype(F32)

    def tile(index, carry):
        base = (index * LANES).astype(F32) - half
        x_all = lanes + base
        totals = [jnp.zeros((slices, LANES), F32) for _ in range(ROW_DEV)]
        for view in range(view_count):
            cosine = cos_ref[first_view + view]
            sine = sin_ref[first_view + view]
            center = shift_ref[view].astype(F32) + ((bins - 1) / 2.0 + MARGIN)
            along = x_all * cosine
            ends = jnp.minimum(base * cosine, (base + (LANES - 1.0)) * cosine)
            for row in range(ROW_DEV):
                y = (row_base + row).astype(F32) - (image_rows - 1) / 2.0
                lift = y * sine
                place = (along + lift) + center
                block = ((ends + lift + center - 0.01) * (1.0 / LANES)).astype(jnp.int32)
                start = pl.multiple_of(block * LANES, LANES)
                lower = jnp.floor(place)
                fraction = place - lower
                weight_low = (1.0 - fraction).astype(BF16).astype(F32)
                weight_high = fraction.astype(BF16).astype(F32)
                spot = lower.astype(jnp.int32) - start
                near = spot < LANES
                inner = spot & (LANES - 1)
                rows = slice(view * slices, (view + 1) * slices)
                take = functools.partial(jnp.take_along_axis, indices=inner, axis=1, mode="promise_in_bounds")
                after = pl.multiple_of(start + LANES, LANES)
                low = jnp.where(near, take(low_ref[rows, pl.ds(start, LANES)]),
                                take(low_ref[rows, pl.ds(after, LANES)]))
                high = jnp.where(near, take(high_ref[rows, pl.ds(start, LANES)]),
                                 take(high_ref[rows, pl.ds(after, LANES)]))
                totals[row] = totals[row] + (low * weight_low + high * weight_high)
        for row in range(ROW_DEV):
            part_ref[row * slices:(row + 1) * slices, pl.ds(pl.multiple_of(index * LANES, LANES), LANES)] = totals[row]
        return carry

    lax.fori_loop(0, width // LANES, tile, 0)
    span = width // QUARTERS
    gathered = jnp.concatenate([part_ref[:, q * span:(q + 1) * span] for q in range(QUARTERS)], axis=0).astype(BF16)
    out_ref[...] = dot(perm_out_ref[...], gathered).astype(BF16).reshape(out_ref.shape)


def exchange_kernel(views, row_groups, scale, part_ref, out_ref, recv_ref, own_ref, up_ref, down_ref,
                    send_sem, recv_sem, halo_send, halo_recv):
    me = lax.axis_index("views")
    group = lax.axis_index("rows")
    above = lax.rem(group + row_groups - 1, row_groups)
    below = lax.rem(group + 1, row_groups)
    barrier = pltpu.get_barrier_semaphore()
    for step in range(1, views):
        pl.semaphore_signal(barrier, inc=1, device_id={"views": lax.rem(me + step, views)}, device_id_type=MESH)
    for other in (above, below):
        pl.semaphore_signal(barrier, inc=1, device_id={"rows": other}, device_id_type=MESH)
    pl.semaphore_wait(barrier, views + 1)
    group_slices = part_ref.shape[0] // views
    copies = []
    for step in range(1, views):
        peer = lax.rem(me + step, views)
        copy = pltpu.make_async_remote_copy(
            src_ref=part_ref.at[pl.ds(peer * group_slices, group_slices)], dst_ref=recv_ref.at[step - 1],
            send_sem=send_sem.at[step - 1], recv_sem=recv_sem.at[step - 1],
            device_id={"views": peer}, device_id_type=MESH)
        copy.start()
        copies.append(copy)
    total = part_ref[pl.ds(me * group_slices, group_slices)].astype(F32)
    for step, copy in enumerate(copies):
        copy.wait_recv()
        total = total + recv_ref[step].astype(F32)
    image = (total * scale).astype(BF16).astype(F32)
    own_ref[...] = image
    rows_half = own_ref.shape[1] // 2
    to_above = pltpu.make_async_remote_copy(
        src_ref=own_ref.at[:, pl.ds(0, rows_half)], dst_ref=down_ref, send_sem=halo_send.at[0], recv_sem=halo_recv.at[0],
        device_id={"rows": above}, device_id_type=MESH)
    to_below = pltpu.make_async_remote_copy(
        src_ref=own_ref.at[:, pl.ds(rows_half, rows_half)], dst_ref=up_ref, send_sem=halo_send.at[1], recv_sem=halo_recv.at[1],
        device_id={"rows": below}, device_id_type=MESH)
    to_above.start()
    to_below.start()
    span = own_ref.shape[2]

    def place(index, values, first_row, count):
        for row in range(count):
            for q in range(QUARTERS):
                out_ref[index, first_row + row:first_row + row + 1, q * span:(q + 1) * span] = (
                    values[row * QUARTERS + q:row * QUARTERS + q + 1])

    for index in range(group_slices):
        place(index, image[index], 2, ROW_DEV)
    to_above.wait_recv()
    to_below.wait_recv()
    has_above = (group > 0).astype(F32)
    has_below = (group < row_groups - 1).astype(F32)
    for index in range(group_slices):
        place(index, up_ref[index] * has_above, 0, 2)
        place(index, down_ref[index] * has_below, 2 + ROW_DEV, 2)
    for copy in copies + [to_above, to_below]:
        copy.wait_send()


def conv_kernel(row_groups, rows_ref, one_ref, bias_one_ref, two_ref, bias_two_ref, out_ref):
    group = lax.axis_index("rows")
    width = rows_ref.shape[2]
    channels = out_ref.shape[1]
    source = rows_ref[0]
    column = lax.broadcasted_iota(jnp.int32, (1, width), 1)

    def spread(values):
        left = jnp.where(column == 0, 0.0, pltpu.roll(values, 1, 1))
        right = jnp.where(column == width - 1, 0.0, pltpu.roll(values, width - 1, 1))
        return [left, values, right]

    window = jnp.concatenate(spread(source), axis=0).astype(BF16)
    window = jnp.concatenate([window] * 3, axis=0)
    hidden = jnp.maximum(dot(one_ref[...], window) + bias_one_ref[...], 0.0)
    hidden_rows = ROW_DEV + 2
    line = lax.broadcasted_iota(jnp.int32, (hidden_rows * channels, 1), 0)
    lowest = jnp.where(group > 0, 0, channels)
    highest = jnp.where(group < row_groups - 1, hidden_rows * channels, (hidden_rows - 1) * channels)
    hidden = jnp.where((line >= lowest) & (line < highest), hidden, 0.0)
    stacked = jnp.concatenate([piece.astype(BF16) for piece in spread(hidden)], axis=0)
    mixed = jnp.maximum(dot(two_ref[...], stacked) + bias_two_ref[...], 0.0)
    out_ref[0] = mixed.reshape(channels, ROW_DEV, width).astype(BF16)


def spread_one(conv_one):
    channels = conv_one.shape[1]
    hidden_rows = ROW_DEV + 2
    taps = conv_one.reshape(3, 3, channels).transpose(2, 1, 0)
    rows = [jnp.pad(taps, ((0, 0), (0, 0), (r, hidden_rows - 1 - r))) for r in range(hidden_rows)]
    full = jnp.stack(rows, axis=0).reshape(hidden_rows * channels, 3 * (hidden_rows + 2))
    return jnp.concatenate(split_parts(full, 3), axis=1)


def spread_two(conv_two):
    channels = conv_two.shape[0]
    taps = conv_two.reshape(channels, 3, 3, channels).transpose(0, 2, 1, 3)
    rows = [jnp.pad(taps, ((0, 0), (0, 0), (r, ROW_DEV - 1 - r), (0, 0))) for r in range(ROW_DEV)]
    return jnp.stack(rows, axis=1).reshape(channels * ROW_DEV, 3 * (ROW_DEV + 2) * channels)


def local(sinogram, view_shift, conv_one, bias_one, conv_two, bias_two):
    slices, view_count, bins = sinogram.shape
    views = lax.axis_size("views")
    row_groups = lax.axis_size("rows")
    views_total = view_count * views
    image_rows = ROW_DEV * row_groups
    channels = conv_one.shape[1]
    flat = slices * view_count
    group_slices = slices // views
    extended = bins + 2 * MARGIN
    span = bins // QUARTERS

    angles = (np.arange(views_total, dtype=np.float32) * np.float32(math.pi / views_total)).astype(np.float64)
    cosines = jnp.asarray(np.cos(angles).astype(np.float32))
    sines = jnp.asarray(np.sin(angles).astype(np.float32))
    order = np.arange(flat).reshape(slices, view_count).T.reshape(-1)
    perm_in = np.zeros((flat, flat), np.float32)
    perm_in[np.arange(flat), order] = 1.0
    size = QUARTERS * ROW_DEV * slices
    order = np.arange(size).reshape(QUARTERS, ROW_DEV, slices).transpose(2, 1, 0).reshape(-1)
    perm_out = np.zeros((size, size), np.float32)
    perm_out[np.arange(size), order] = 1.0

    vmem = pl.BlockSpec(memory_space=pltpu.VMEM)
    smem = pl.BlockSpec(memory_space=pltpu.SMEM)
    partial = pl.pallas_call(
        functools.partial(project_kernel, views_total, image_rows),
        out_shape=jax.ShapeDtypeStruct((slices, QUARTERS * ROW_DEV, span), BF16),
        in_specs=[vmem] * 3 + [smem] * 3,
        out_specs=vmem,
        scratch_shapes=[
            pltpu.VMEM((bins // BLOCK * flat, BLOCK), F32),
            pltpu.VMEM((flat, extended), F32),
            pltpu.VMEM((flat, extended), F32),
            pltpu.VMEM((ROW_DEV * slices, bins), F32),
        ],
        name="project",
    )(sinogram, jnp.asarray(perm_in, dtype=BF16), jnp.asarray(perm_out, dtype=BF16), view_shift, cosines, sines)

    halo = pltpu.VMEM((group_slices, QUARTERS * ROW_DEV // 2, span), F32)
    rows = pl.pallas_call(
        functools.partial(exchange_kernel, views, row_groups, math.pi / views_total),
        out_shape=jax.ShapeDtypeStruct((group_slices, ROW_DEV + 4, bins), F32),
        in_specs=[vmem],
        out_specs=vmem,
        scratch_shapes=[
            pltpu.VMEM((views - 1, group_slices, QUARTERS * ROW_DEV, span), BF16),
            pltpu.VMEM((group_slices, QUARTERS * ROW_DEV, span), F32),
            halo,
            halo,
            pltpu.SemaphoreType.DMA((views - 1,)),
            pltpu.SemaphoreType.DMA((views - 1,)),
            pltpu.SemaphoreType.DMA((2,)),
            pltpu.SemaphoreType.DMA((2,)),
        ],
        compiler_params=pltpu.CompilerParams(collective_id=0, has_side_effects=True),
        name="exchange",
    )(partial)

    hidden_rows = ROW_DEV + 2
    one = spread_one(conv_one)
    two = spread_two(conv_two)
    one_bias = jnp.tile(bias_one, hidden_rows)[:, None]
    two_bias = jnp.repeat(bias_two, ROW_DEV)[:, None]
    conv = pl.pallas_call(
        functools.partial(conv_kernel, row_groups),
        grid=(group_slices,),
        out_shape=jax.ShapeDtypeStruct((group_slices, channels, ROW_DEV, bins), BF16),
        in_specs=[pl.BlockSpec((1, ROW_DEV + 4, bins), lambda i: (i, 0, 0))] + [vmem] * 4,
        out_specs=pl.BlockSpec((1, channels, ROW_DEV, bins), lambda i: (i, 0, 0, 0)),
        name="conv",
    )
    return conv(rows, one, one_bias, two, two_bias)


def solution(mesh):
    return jax.shard_map(
        local,
        mesh=mesh,
        in_specs=(P(None, "views", None), P("views"), P(), P(), P(), P()),
        out_specs=P("views", None, "rows", None),
        check_vma=False,
    )
```

time: 220 us -> 31.8 us (0.14)
  waiting for transfers between devices: 73.7 us -> 0 us
  matrix products: 47.7 us -> 0 us
  loops' own time: 47 us -> 0 us
  Pallas kernels: 0 us -> 25.6 us
  local copies, waits for them, and re-layouts: 18.6 us -> 4.35 us
  between operations: 13.6 us -> 0.1 us
  other arithmetic: 10.8 us -> 1.55 us
  starting transfers between devices: 7.42 us -> 0 us
    unnamed x2 -> x0, waiting for transfers between devices: 70.7 us -> none
    dot_general x66 -> x0, matrix products: 47.7 us -> none  [the longest x64 27.1 us: one_view(): jnp.einsum('rtb,sb->srt', weights, band, preferred_element_type=jnp.float32)]
    another operation x1 -> x0, loops' own time: 47 us -> none  [backproject(): return lax.fori_loop(0, view_count, one_view, start)]
    pallas_call x0 -> x3, Pallas kernels: none -> 25.6 us  [the longest x1 13.5 us: local(): pl.pallas_call(functools.partial(exchange_kernel, views, row_groups, math...]
    unnamed x24 -> x6, local copies, waits for them, and re-layouts: 10.9 us -> 0.03 us
    ppermute x2 -> x0, starting transfers between devices: 7.42 us -> none  [the longest x1 5.5 us: extended_2(): lax.ppermute(tail, axis, [(i, (i + 1) % count) for i in range(ends)])]
    reduce_min x8 -> x0, other arithmetic: 6.2 us -> none  [one_view(): lowest = jnp.min(position)]
    dynamic_slice x8 -> x0, local copies, waits for them, and re-layouts: 4.64 us -> none  [one_view(): shift = lax.dynamic_index_in_dim(view_shift, view, 0, keepdims=False)]
  transfers between devices with their start and end apart: 3 -> 0, of which waited for: 2 -> 0; matrix products, arithmetic and copies ran while one was open for 0% -> 0% of each run, Pallas kernels for 0% -> 0%
where the time goes in v1:
time: 31.8 us; the launch traced here: 31.6 us
  Pallas kernels  25.6 us (81%)
  local copies, waits for them, and re-layouts  4.35 us (14%)
  other arithmetic  1.55 us (5%)
    pallas_call x1, Pallas kernels, local(): pl.pallas_call(functools.partial(exchange_kernel, views, row_groups, math...  13.5 us
    pallas_call x1, Pallas kernels, local(): pl.pallas_call(functools.partial(project_kernel, views_total, image_rows)...  8.95 us
    pallas_call x1, Pallas kernels, local(): return conv(rows, one, one_bias, two, two_bias)  3.18 us
    reshape x1, local copies, waits for them, and re-layouts, spread_two(): jnp.stack(rows, axis=1)  1.1 us
    another operation x1, other arithmetic, spread_two(): jnp.stack(rows, axis=1)  0.81 us
    another operation x2, local copies, waits for them, and re-layouts, local(): one_bias = jnp.tile(bias_one, hidden_rows)[:, None]  0.76 us
    concatenate x1, other arithmetic, spread_one(): return jnp.concatenate(split_parts(full, 3), axis=1)  0.71 us
    reshape x2, local copies, waits for them, and re-layouts, spread_one(): taps = conv_one.reshape(3, 3, channels).transpose(2, 1, 0)  0.71 us

profile of v1, /device:TPU:1, one launch (start us, length us, event | category | flops | bytes accessed | tf_op | source)
XLA Modules:
  0.0 31.6 jit_solution(18230311362825459208)
XLA Ops:
  0.0 0.7 %reshape.13 = f32[3,3,32]{2,1,0:T(4,128)S(1)} reshape(f32[9,32]{1,0:T(8,128)} %param.12) | data formatting | bytes 2304 | tf_op jit(solution)/shard_map/reshape | solution.py:213
  0.7 0.1 stack.42
  0.8 0.1 reshape.14
  0.9 0.1 copy.36
  1.1 0.1 copy.35
  1.2 0.0 copy-start
  1.2 0.7 %pad_maximum_fusion.1.one_ref = bf16[192,72]{1,0:T(8,128)(2,1)} fusion(bf16[192,24]{1,0:T(8,128)(2,1)S(1)} %get-tuple-element.6, bf16[192,24]{1,0:T(8,128)(2,1)S(1)} %get-tuple-element.5, bf16[192,24]{1,0:T(8,128)(2,1)S(1)} %copy.36), kind=kLoop, calls=%fused_computation.8 | loop fusion | flops 82944 | bytes 55296 | tf_op jit(solution)/shard_map/concatenate | solution.py:216
  1.9 0.0 copy-done
  1.9 0.1 reshape.15
  2.1 0.3 pad_bitcast_fusion.3
  2.3 0.8 %pad_maximum_fusion = bf16[32,4,3,6,32]{4,2,3,0,1:T(4,128)(2,1)S(1)} fusion(bf16[32,1,3,6,32]{4,2,3,0,1:T(4,128)(2,1)S(1)} %get-tuple-element.8, bf16[32,1,3,6,32]{4,2,3,0,1:T(4,128)(2,1)S(1)} %get-tuple-element.9, bf16[32,1,3,6,32]{4,2,3,0,1:T(4,128)(2,1)S(1)} %get-tuple-element.10, bf16[32,1,3,6,32]{4,2,3,0,1:T(4,128)(2,1)S(1)} %get-tuple-element.7), kind=kLoop, calls=%fused_computation | loop fusion | flops 221184 | bytes 294912 | tf_op jit(solution)/shard_map/stack | solution.py:223
  3.1 0.2 copy.37
  3.3 1.1 %reshape.16.two_ref = bf16[128,576]{1,0:T(8,128)(2,1)} reshape(bf16[32,4,3,6,32]{4,3,2,1,0:T(8,128)(2,1)S(1)} %copy.37) | data formatting | bytes 294912 | tf_op jit(solution)/shard_map/reshape | solution.py:223
  4.4 8.9 %project.1.part_ref = bf16[8,16,512]{2,1,0:T(8,128)(2,1)} custom-call(bf16[8,8,2048]{2,1,0:T(8,128)(2,1)} %sino_ref.1, bf16[64,64]{1,0:T(8,128)(2,1)} %constant.15.clone.perm_in_ref, bf16[128,128]{1,0:T(8,128)(2,1)} %constant.16.clone.perm_out_ref, s32[8]{0:T(128)} %shift_ref.1, f32[64]{0:T(128)} %constant.13.clone.cos_ref, f32[64]{0:T(128)} %constant.14.clone.sin_ref), custom_call_target="tpu_custom_call" | custom-call | tf_op jit(solution)/shard_map/project/pallas_call | solution.py:251
  13.4 0.0 copy-start.1
  13.4 13.5 %exchange.1.rows_ref = f32[1,8,2048]{2,1,0:T(8,128)} custom-call(bf16[8,16,512]{2,1,0:T(8,128)(2,1)} %project.1.part_ref), custom_call_target="tpu_custom_call" | custom-call | tf_op jit(solution)/shard_map/exchange/pallas_call | solution.py:266
  26.8 0.0 copy-done.1
  26.9 0.0 copy-start.2
  26.9 0.8 %broadcast_in_dim_tile.4.bias_one_ref = f32[192,1]{1,0:T(8,128)} reshape(f32[6,32]{1,0:T(8,128)S(1)} %tile.2) | data formatting | bytes 1536 | tf_op jit(solution)/shard_map/broadcast_in_dim;tile | solution.py:288
  27.6 0.0 copy-done.2
  27.6 0.1 broadcast_in_dim.3
  27.7 0.7 %broadcast_in_dim_reshape.4.bias_two_ref = f32[128,1]{1,0:T(8,128)} reshape(f32[32,4]{1,0:T(8,128)S(1)} %broadcast_in_dim.3) | data formatting | bytes 1024 | tf_op jit(solution)/shard_map/broadcast_in_dim;reshape | solution.py:289
  28.4 3.2 %conv.1 = bf16[1,32,4,2048]{3,2,1,0:T(4,128)(2,1)} custom-call(f32[1,8,2048]{2,1,0:T(8,128)} %exchange.1.rows_ref, bf16[192,72]{1,0:T(8,128)(2,1)} %pad_maximum_fusion.1.one_ref, f32[192,1]{1,0:T(8,128)} %broadcast_in_dim_tile.4.bias_one_ref, bf16[128,576]{1,0:T(8,128)(2,1)} %reshape.16.two_ref, f32[128,1]{1,0:T(8,128)} %broadcast_in_dim_reshape.4.bias_two_ref), custom_call_target="tpu_custom_call" | custom-call | tf_op jit(solution)/shard_map/conv/pallas_call | solution.py:298
  (5 shorter events, 0.0 us)
Async XLA Ops:
  1.2 0.7 %copy-start = (bf16[32,288]{1,0:T(8,128)(2,1)S(1)}, bf16[32,288]{1,0:T(8,128)(2,1)}, u32[]{:S(2)}) copy-start(bf16[32,288]{1,0:T(8,128)(2,1)} %param.14) | copy-start | bytes 55300
  13.4 13.5 %copy-start.1 = (f32[32]{0:T(128)S(1)}, f32[32]{0:T(128)}, u32[]{:S(2)}) copy-start(f32[32]{0:T(128)} %param.13) | copy-start | bytes 388
  26.9 0.8 %copy-start.2 = (f32[32]{0:T(128)S(1)}, f32[32]{0:T(128)}, u32[]{:S(2)}) copy-start(f32[32]{0:T(128)} %param.15) | copy-start | bytes 388

commit v2 on v1

v2 whole, which is shorter than its diff:
```python
import functools
import math

import jax
import jax.numpy as jnp
import numpy as np
from jax import lax
from jax.experimental import pallas as pl
from jax.experimental.pallas import tpu as pltpu
from jax.sharding import PartitionSpec as P

MARGIN = 384
ROW_DEV = 4
LANES = 128
BLOCK = 256
QUARTERS = 4
CHUNKS = 2
FIXED = 18
F32 = jnp.float32
BF16 = jnp.bfloat16
MESH = pl.DeviceIdType.MESH


def split_parts(values, count):
    parts = []
    rest = values
    for part in range(count):
        piece = rest.astype(BF16)
        parts.append(piece)
        if part + 1 < count:
            rest = rest - piece.astype(F32)
    return parts


def ramp_block(block_offset):
    rows = lax.broadcasted_iota(jnp.int32, (BLOCK, BLOCK), 0)
    cols = lax.broadcasted_iota(jnp.int32, (BLOCK, BLOCK), 1)
    offset = cols - rows + block_offset * BLOCK
    square = (offset * offset).astype(F32)
    taps = jnp.where((offset & 1) != 0, (-1.0 / (math.pi * math.pi)) / jnp.maximum(square, 1.0), 0.0)
    if block_offset == 0:
        taps = jnp.where(offset == 0, 0.25, taps)
    return taps


def dot(a, b):
    return lax.dot_general(a, b, (((1,), (0,)), ((), ())), preferred_element_type=F32)


def dot_t(a, b):
    return lax.dot_general(a, b, (((1,), (1,)), ((), ())), preferred_element_type=F32)


def tap_matrices(one_ref, bias_one_ref, two_ref, bias_two_ref, expand_ref):
    channels = one_ref.shape[1]
    hidden_rows = ROW_DEV + 2
    image_lines = ROW_DEV + 4
    lanes = hidden_rows * channels
    rep = jnp.concatenate([one_ref[...]] * hidden_rows, axis=1)
    line = lax.broadcasted_iota(jnp.int32, (3 * image_lines, lanes), 0) % image_lines
    target = lax.broadcasted_iota(jnp.int32, (3 * image_lines, lanes), 1) // channels
    full = jnp.zeros((3 * image_lines, lanes), F32)
    for i in range(3):
        picked = jnp.concatenate(
            [jnp.broadcast_to(rep[3 * i + dx:3 * i + dx + 1], (image_lines, lanes)) for dx in range(3)], axis=0)
        full = full + jnp.where(line - target == i, picked, 0.0)
    bias = jnp.concatenate([bias_one_ref[...]] * hidden_rows, axis=1)
    bias_parts = [piece.astype(F32) for piece in split_parts(bias, 3)]
    bias_rows = jnp.concatenate(bias_parts + [jnp.zeros((5, lanes), F32)], axis=0)
    pieces = [piece.astype(F32) for piece in split_parts(full, 3)]
    one = jnp.concatenate(pieces + [bias_rows], axis=0).T.astype(BF16)
    taps = two_ref[...].astype(F32)
    depth = 3 * hidden_rows * channels
    rows = channels * ROW_DEV
    out_row = lax.broadcasted_iota(jnp.int32, (rows, depth), 0) % ROW_DEV
    hidden_row = (lax.broadcasted_iota(jnp.int32, (rows, depth), 1) // channels) % hidden_rows
    two = jnp.zeros((rows, depth), F32)
    for i in range(3):
        wide = jnp.concatenate(
            [taps[:, (3 * i + dx) * channels:(3 * i + dx + 1) * channels] for dx in range(3) for _ in range(hidden_rows)],
            axis=1)
        two = two + jnp.where(hidden_row - out_row == i, dot(expand_ref[...], wide.astype(BF16)), 0.0)
    second = sum(dot_t(expand_ref[...], jnp.broadcast_to(piece.astype(F32), (LANES, channels)).astype(BF16))
                 for piece in split_parts(bias_two_ref[...], 3))
    return one, two.astype(BF16), second


def project_kernel(views, row_groups, sino_ref, perm_in_ref, perm_out_ref, expand_ref, shift_ref, cos_ref, sin_ref, fixed_cos_ref, fixed_sin_ref,
                   conv_one_ref, bias_one_ref, conv_two_ref, bias_two_ref,
                   out_ref, one_ref, two_ref, second_ref,
                   sum_ref, low_ref, high_ref, part_ref, send_ref, recv_ref, own_ref, up_ref, down_ref,
                   send_sem, recv_sem, halo_send, halo_recv):
    me = lax.axis_index("views")
    group = lax.axis_index("rows")
    above = lax.rem(group + row_groups - 1, row_groups)
    below = lax.rem(group + 1, row_groups)
    barrier = pltpu.get_barrier_semaphore()
    for step in range(1, views):
        pl.semaphore_signal(barrier, inc=1, device_id={"views": lax.rem(me + step, views)}, device_id_type=MESH)
    for other in (above, below):
        pl.semaphore_signal(barrier, inc=1, device_id={"rows": other}, device_id_type=MESH)

    slices, view_count, bins = sino_ref.shape
    width = bins
    flat = slices * view_count
    blocks = bins // BLOCK
    views_total = view_count * views
    image_rows = ROW_DEV * row_groups
    scale = math.pi / views_total
    ordered = dot(perm_in_ref[...], sino_ref[...].reshape(flat, bins)).astype(BF16)
    stacked = jnp.concatenate([ordered[:, k * BLOCK:(k + 1) * BLOCK] for k in range(blocks)], axis=0)
    for step in range(blocks):
        parts = split_parts(ramp_block(step), 3 if step < 2 else 2)
        count = (blocks - step) * flat
        down = stacked[:count]
        forward = sum(dot(down, part) for part in parts[::-1])
        if step == 0:
            sum_ref[...] = forward
        else:
            sum_ref[pl.ds(step * flat, count), :] += forward
            up = stacked[step * flat:]
            backward = sum(dot_t(up, part) for part in parts[::-1])
            sum_ref[pl.ds(0, count), :] += backward
    zeros = jnp.zeros((flat, MARGIN), F32)
    filtered = [sum_ref[k * flat:(k + 1) * flat, :].astype(BF16).astype(F32) for k in range(blocks)]
    padded = jnp.concatenate([zeros] + filtered + [zeros], axis=1)
    shifted = pltpu.roll(padded, padded.shape[1] - 1, 1)
    for block in range(low_ref.shape[0]):
        low_ref[block] = padded[:, block * LANES:(block + 1) * LANES]
        high_ref[block] = shifted[:, block * LANES:(block + 1) * LANES]

    first_view = me * view_count
    row_base = group * ROW_DEV
    half = (width - 1) / 2.0
    lanes = lax.broadcasted_iota(jnp.int32, (slices, LANES), 1).astype(F32)
    chunk_cols = width // CHUNKS
    fixed_half = (1 << FIXED) - (1 << (FIXED - 4))
    span = chunk_cols // QUARTERS
    group_slices = slices // views

    def tile(chunk, index, carry):
        base = (index * LANES + chunk * chunk_cols).astype(F32) - half
        x_all = lanes + base
        twice_base = 2 * (index * LANES + chunk * chunk_cols) - (width - 1)
        totals = [jnp.zeros((slices, LANES), F32) for _ in range(ROW_DEV)]
        for view in range(view_count):
            cosine = cos_ref[first_view + view]
            sine = sin_ref[first_view + view]
            center = shift_ref[view].astype(F32) + ((bins - 1) / 2.0 + MARGIN)
            along = x_all * cosine
            fixed_cos = fixed_cos_ref[first_view + view]
            fixed_sin = fixed_sin_ref[first_view + view]
            ends = jnp.minimum(twice_base * fixed_cos, (twice_base + 2 * (LANES - 1)) * fixed_cos) + fixed_half
            origin = shift_ref[view] + ((bins - 1) // 2 + MARGIN)
            for row in range(ROW_DEV):
                y = (row_base + row).astype(F32) - (image_rows - 1) / 2.0
                lift = y * sine
                place = (along + lift) + center
                twice_y = 2 * (row_base + row) - (image_rows - 1)
                lowest = ((ends + twice_y * fixed_sin) >> (FIXED + 1)) + origin
                block = lowest >> 7
                lower = jnp.floor(place)
                fraction = place - lower
                weight_low = (1.0 - fraction).astype(BF16).astype(F32)
                weight_high = fraction.astype(BF16).astype(F32)
                spot = lower.astype(jnp.int32) - block * LANES
                near = spot < LANES
                inner = spot & (LANES - 1)
                rows = slice(view * slices, (view + 1) * slices)
                take = functools.partial(jnp.take_along_axis, indices=inner, axis=1, mode="promise_in_bounds")
                low = jnp.where(near, take(low_ref[block, rows]), take(low_ref[block + 1, rows]))
                high = jnp.where(near, take(high_ref[block, rows]), take(high_ref[block + 1, rows]))
                totals[row] = totals[row] + (low * weight_low + high * weight_high)
        for row in range(ROW_DEV):
            part_ref[row * slices:(row + 1) * slices, pl.ds(pl.multiple_of(index * LANES, LANES), LANES)] = totals[row]
        return carry

    copies = []
    for chunk in range(CHUNKS):
        lax.fori_loop(0, chunk_cols // LANES, functools.partial(tile, chunk), 0)
        gathered = jnp.concatenate([part_ref[:, q * span:(q + 1) * span] for q in range(QUARTERS)], axis=0).astype(BF16)
        send_ref[chunk] = dot(perm_out_ref[...], gathered).astype(BF16).reshape(slices, QUARTERS * ROW_DEV, span)
        if chunk == 0:
            pl.semaphore_wait(barrier, views + 1)
        sent = []
        for step in range(1, views):
            peer = lax.rem(me + step, views)
            slot = chunk * (views - 1) + step - 1
            copy = pltpu.make_async_remote_copy(
                src_ref=send_ref.at[chunk, pl.ds(peer * group_slices, group_slices)], dst_ref=recv_ref.at[slot],
                send_sem=send_sem.at[slot], recv_sem=recv_sem.at[slot],
                device_id={"views": peer}, device_id_type=MESH)
            copy.start()
            sent.append((slot, copy))
        copies.append(sent)

    one, two, second = tap_matrices(conv_one_ref, bias_one_ref, conv_two_ref, bias_two_ref, expand_ref)
    one_ref[...] = one
    two_ref[...] = two
    second_ref[...] = second

    def place_rows(index, chunk, values, first_row, count):
        for row in range(count):
            for q in range(QUARTERS):
                column = chunk * chunk_cols + q * span
                out_ref[index, first_row + row:first_row + row + 1, column:column + span] = (
                    values[row * QUARTERS + q:row * QUARTERS + q + 1])

    rows_half = QUARTERS * ROW_DEV // 2
    halos = []
    for chunk in range(CHUNKS):
        total = send_ref[chunk, pl.ds(me * group_slices, group_slices)].astype(F32)
        for slot, copy in copies[chunk]:
            copy.wait_recv()
            total = total + recv_ref[slot].astype(F32)
        image = (total * scale).astype(BF16).astype(F32)
        own_ref[chunk] = image
        to_above = pltpu.make_async_remote_copy(
            src_ref=own_ref.at[chunk, :, pl.ds(0, rows_half)], dst_ref=down_ref.at[chunk],
            send_sem=halo_send.at[2 * chunk], recv_sem=halo_recv.at[2 * chunk],
            device_id={"rows": above}, device_id_type=MESH)
        to_below = pltpu.make_async_remote_copy(
            src_ref=own_ref.at[chunk, :, pl.ds(rows_half, rows_half)], dst_ref=up_ref.at[chunk],
            send_sem=halo_send.at[2 * chunk + 1], recv_sem=halo_recv.at[2 * chunk + 1],
            device_id={"rows": below}, device_id_type=MESH)
        to_above.start()
        to_below.start()
        halos.append((to_above, to_below))
        for index in range(group_slices):
            place_rows(index, chunk, image[index], 2, ROW_DEV)
    has_above = (group > 0).astype(F32)
    has_below = (group < row_groups - 1).astype(F32)
    for chunk, (to_above, to_below) in enumerate(halos):
        to_above.wait_recv()
        to_below.wait_recv()
        for index in range(group_slices):
            place_rows(index, chunk, up_ref[chunk, index] * has_above, 0, 2)
            place_rows(index, chunk, down_ref[chunk, index] * has_below, 2 + ROW_DEV, 2)
    for sent in copies:
        for _, copy in sent:
            copy.wait_send()
    for pair in halos:
        for copy in pair:
            copy.wait_send()


def conv_kernel(row_groups, rows_ref, one_ref, two_ref, second_ref, out_ref):
    group = lax.axis_index("rows")
    width = rows_ref.shape[2]
    channels = out_ref.shape[1]
    source = rows_ref[0]
    column = lax.broadcasted_iota(jnp.int32, (1, width), 1)

    def spread(values):
        left = jnp.where(column == 0, 0.0, pltpu.roll(values, 1, 1))
        right = jnp.where(column == width - 1, 0.0, pltpu.roll(values, width - 1, 1))
        return [left, values, right]

    window = jnp.concatenate(spread(source), axis=0).astype(BF16)
    window = jnp.concatenate([window] * 3 + [jnp.ones((8, width), BF16)], axis=0)
    hidden = jnp.maximum(dot(one_ref[...], window), 0.0)
    hidden_rows = ROW_DEV + 2
    line = lax.broadcasted_iota(jnp.int32, (hidden_rows * channels, 1), 0)
    lowest = jnp.where(group > 0, 0, channels)
    highest = jnp.where(group < row_groups - 1, hidden_rows * channels, (hidden_rows - 1) * channels)
    hidden = jnp.where((line >= lowest) & (line < highest), hidden, 0.0)
    stacked = jnp.concatenate([piece.astype(BF16) for piece in spread(hidden)], axis=0)
    mixed = jnp.maximum(dot(two_ref[...], stacked) + second_ref[:, :1], 0.0)
    out_ref[0] = mixed.reshape(channels, ROW_DEV, width).astype(BF16)


def local(sinogram, view_shift, conv_one, bias_one, conv_two, bias_two):
    slices, view_count, bins = sinogram.shape
    views = lax.axis_size("views")
    row_groups = lax.axis_size("rows")
    views_total = view_count * views
    image_rows = ROW_DEV * row_groups
    channels = conv_one.shape[1]
    flat = slices * view_count
    group_slices = slices // views
    extended = bins + 2 * MARGIN
    span = bins // (QUARTERS * CHUNKS)

    angles = (np.arange(views_total, dtype=np.float32) * np.float32(math.pi / views_total)).astype(np.float64)
    cosines = jnp.asarray(np.cos(angles).astype(np.float32))
    sines = jnp.asarray(np.sin(angles).astype(np.float32))
    fixed_cosines = jnp.asarray(np.round(np.cos(angles) * (1 << FIXED)).astype(np.int32))
    fixed_sines = jnp.asarray(np.round(np.sin(angles) * (1 << FIXED)).astype(np.int32))
    order = np.arange(flat).reshape(slices, view_count).T.reshape(-1)
    perm_in = np.zeros((flat, flat), np.float32)
    perm_in[np.arange(flat), order] = 1.0
    size = QUARTERS * ROW_DEV * slices
    order = np.arange(size).reshape(QUARTERS, ROW_DEV, slices).transpose(2, 1, 0).reshape(-1)
    perm_out = np.zeros((size, size), np.float32)
    perm_out[np.arange(size), order] = 1.0

    expand = np.repeat(np.eye(channels, dtype=np.float32), ROW_DEV, axis=0)

    vmem = pl.BlockSpec(memory_space=pltpu.VMEM)
    smem = pl.BlockSpec(memory_space=pltpu.SMEM)
    hidden_rows = ROW_DEV + 2
    halo = pltpu.VMEM((CHUNKS, group_slices, QUARTERS * ROW_DEV // 2, span), F32)
    slots = CHUNKS * (views - 1)
    rows, one, two, second = pl.pallas_call(
        functools.partial(project_kernel, views, row_groups),
        out_shape=(
            jax.ShapeDtypeStruct((group_slices, ROW_DEV + 4, bins), F32),
            jax.ShapeDtypeStruct((hidden_rows * channels, 9 * (ROW_DEV + 4) + 8), BF16),
            jax.ShapeDtypeStruct((channels * ROW_DEV, 3 * hidden_rows * channels), BF16),
            jax.ShapeDtypeStruct((channels * ROW_DEV, LANES), F32),
        ),
        in_specs=[vmem] * 4 + [smem] * 5 + [vmem] * 4,
        out_specs=(vmem,) * 4,
        scratch_shapes=[
            pltpu.VMEM((bins // BLOCK * flat, BLOCK), F32),
            pltpu.VMEM((extended // LANES, flat, LANES), F32),
            pltpu.VMEM((extended // LANES, flat, LANES), F32),
            pltpu.VMEM((ROW_DEV * slices, bins // CHUNKS), F32),
            pltpu.VMEM((CHUNKS, slices, QUARTERS * ROW_DEV, span), BF16),
            pltpu.VMEM((slots, group_slices, QUARTERS * ROW_DEV, span), BF16),
            pltpu.VMEM((CHUNKS, group_slices, QUARTERS * ROW_DEV, span), F32),
            halo,
            halo,
            pltpu.SemaphoreType.DMA((slots,)),
            pltpu.SemaphoreType.DMA((slots,)),
            pltpu.SemaphoreType.DMA((2 * CHUNKS,)),
            pltpu.SemaphoreType.DMA((2 * CHUNKS,)),
        ],
        compiler_params=pltpu.CompilerParams(collective_id=0, has_side_effects=True),
        name="project",
    )(sinogram, jnp.asarray(perm_in, dtype=BF16), jnp.asarray(perm_out, dtype=BF16), jnp.asarray(expand, dtype=BF16),
      view_shift, cosines, sines, fixed_cosines, fixed_sines, conv_one, bias_one[None, :], conv_two, bias_two[None, :])

    conv = pl.pallas_call(
        functools.partial(conv_kernel, row_groups),
        grid=(group_slices,),
        out_shape=jax.ShapeDtypeStruct((group_slices, channels, ROW_DEV, bins), BF16),
        in_specs=[pl.BlockSpec((1, ROW_DEV + 4, bins), lambda i: (i, 0, 0))] + [vmem] * 3,
        out_specs=pl.BlockSpec((1, channels, ROW_DEV, bins), lambda i: (i, 0, 0, 0)),
        name="conv",
    )
    return conv(rows, one, two, second)


def solution(mesh):
    return jax.shard_map(
        local,
        mesh=mesh,
        in_specs=(P(None, "views", None), P("views"), P(), P(), P(), P()),
        out_specs=P("views", None, "rows", None),
        check_vma=False,
    )
```

time: 31.8 us -> 23.2 us (0.73)
  local copies, waits for them, and re-layouts: 4.35 us -> 0 us
  Pallas kernels: 25.6 us -> 23.1 us
  other arithmetic: 1.55 us -> 0 us
    pallas_call x3 -> x2, Pallas kernels: 25.6 us -> 23.1 us  [the longest x1 20 us: local(): pl.pallas_call(functools.partial(project_kernel, views, row_groups), out_...]
    reshape x6 -> x0, local copies, waits for them, and re-layouts: 2.1 us -> none  [the longest x1 1.1 us: spread_two(): jnp.stack(rows, axis=1)]
    another operation x6 -> x0, local copies, waits for them, and re-layouts: 2.02 us -> none  [the longest x2 0.76 us: local(): one_bias = jnp.tile(bias_one, hidden_rows)[:, None]]
    another operation x1 -> x0, other arithmetic: 0.81 us -> none  [spread_two(): jnp.stack(rows, axis=1)]
    concatenate x1 -> x0, other arithmetic: 0.71 us -> none  [spread_one(): return jnp.concatenate(split_parts(full, 3), axis=1)]
where the time goes in v2:
time: 23.2 us; the launch traced here: 23.1 us
  Pallas kernels  23.1 us (100%)
    pallas_call x1, Pallas kernels, local(): pl.pallas_call(functools.partial(project_kernel, views, row_groups), out_...  20 us
    pallas_call x1, Pallas kernels, local(): return conv(rows, one, two, second)  3.05 us

profile of v2, /device:TPU:1, one launch (start us, length us, event | category | flops | bytes accessed | tf_op | source)
XLA Modules:
  0.0 23.1 jit_solution(5333485168837794420)
XLA Ops:
  0.0 20.0 %project.1 = (f32[1,8,2048]{2,1,0:T(8,128)}, bf16[192,80]{1,0:T(8,128)(2,1)}, bf16[128,576]{1,0:T(8,128)(2,1)}, f32[128,128]{1,0:T(8,128)}) custom-call(bf16[8,8,2048]{2,1,0:T(8,128)(2,1)} %sino_ref.1, bf16[64,64]{1,0:T(8,128)(2,1)} %constant.18.clone.perm_in_ref, bf16[128,128]{1,0:T(8,128)(2,1)} %constant.19.clone.perm_out_ref, ...), custom_call_target="tpu_custom_call" | custom-call | tf_op jit(solution)/shard_map/project/pallas_call | solution.py:304
  20.0 3.1 %conv.1 = bf16[1,32,4,2048]{3,2,1,0:T(4,128)(2,1)} custom-call(f32[1,8,2048]{2,1,0:T(8,128)} %get-tuple-element.9.rows_ref, bf16[192,80]{1,0:T(8,128)(2,1)} %get-tuple-element.10.one_ref, bf16[128,576]{1,0:T(8,128)(2,1)} %get-tuple-element.11.two_ref, f32[128,128]{1,0:T(8,128)} %get-tuple-element.12.second_ref), custom_call_target="tpu_custom_call" | custom-call | tf_op jit(solution)/shard_map/conv/pallas_call | solution.py:342

commit v3 on v2

--- a/solution.py
+++ b/solution.py
@@ -16,6 +16,7 @@
 QUARTERS = 4
 CHUNKS = 2
 FIXED = 18
+WINDOW = 64
 F32 = jnp.float32
 BF16 = jnp.bfloat16
 MESH = pl.DeviceIdType.MESH
@@ -32,15 +33,19 @@
     return parts
 
 
-def ramp_block(block_offset):
+def ramp_base():
     rows = lax.broadcasted_iota(jnp.int32, (BLOCK, BLOCK), 0)
     cols = lax.broadcasted_iota(jnp.int32, (BLOCK, BLOCK), 1)
-    offset = cols - rows + block_offset * BLOCK
-    square = (offset * offset).astype(F32)
-    taps = jnp.where((offset & 1) != 0, (-1.0 / (math.pi * math.pi)) / jnp.maximum(square, 1.0), 0.0)
+    offset = cols - rows
+    return offset.astype(F32), jnp.where((offset & 1) != 0, -1.0 / (math.pi * math.pi), 0.0)
+
+
+def ramp_block(base, numerator, block_offset):
+    offset = base + float(block_offset * BLOCK)
+    square = offset * offset
     if block_offset == 0:
-        taps = jnp.where(offset == 0, 0.25, taps)
-    return taps
+        return jnp.where(base == 0.0, 0.25, numerator / jnp.maximum(square, 1.0))
+    return numerator / square
 
 
 def dot(a, b):
@@ -109,8 +114,9 @@
     scale = math.pi / views_total
     ordered = dot(perm_in_ref[...], sino_ref[...].reshape(flat, bins)).astype(BF16)
     stacked = jnp.concatenate([ordered[:, k * BLOCK:(k + 1) * BLOCK] for k in range(blocks)], axis=0)
+    base_offset, numerator = ramp_base()
     for step in range(blocks):
-        parts = split_parts(ramp_block(step), 3 if step < 2 else 2)
+        parts = split_parts(ramp_block(base_offset, numerator, step), 3 if step < 2 else 1)
         count = (blocks - step) * flat
         down = stacked[:count]
         forward = sum(dot(down, part) for part in parts[::-1])
@@ -124,10 +130,12 @@
     zeros = jnp.zeros((flat, MARGIN), F32)
     filtered = [sum_ref[k * flat:(k + 1) * flat, :].astype(BF16).astype(F32) for k in range(blocks)]
     padded = jnp.concatenate([zeros] + filtered + [zeros], axis=1)
-    shifted = pltpu.roll(padded, padded.shape[1] - 1, 1)
-    for block in range(low_ref.shape[0]):
-        low_ref[block] = padded[:, block * LANES:(block + 1) * LANES]
-        high_ref[block] = shifted[:, block * LANES:(block + 1) * LANES]
+    for ref, lead in ((low_ref, 0), (high_ref, 1)):
+        for odd in range(2):
+            turn = odd * WINDOW + lead
+            turned = pltpu.roll(padded, padded.shape[1] - turn, 1) if turn else padded
+            for block in range(ref.shape[0] // 2):
+                ref[2 * block + odd] = turned[:, block * LANES:(block + 1) * LANES]
 
     first_view = me * view_count
     row_base = group * ROW_DEV
@@ -152,24 +160,25 @@
             fixed_sin = fixed_sin_ref[first_view + view]
             ends = jnp.minimum(twice_base * fixed_cos, (twice_base + 2 * (LANES - 1)) * fixed_cos) + fixed_half
             origin = shift_ref[view] + ((bins - 1) // 2 + MARGIN)
+            twice_y = 2 * row_base - (image_rows - 1)
+            window = (((ends + twice_y * fixed_sin) >> (FIXED + 1)) + origin) >> 6
+            rows = slice(view * slices, (view + 1) * slices)
+            low_near, low_far = low_ref[window, rows], low_ref[window + 2, rows]
+            high_near, high_far = high_ref[window, rows], high_ref[window + 2, rows]
             for row in range(ROW_DEV):
                 y = (row_base + row).astype(F32) - (image_rows - 1) / 2.0
                 lift = y * sine
                 place = (along + lift) + center
-                twice_y = 2 * (row_base + row) - (image_rows - 1)
-                lowest = ((ends + twice_y * fixed_sin) >> (FIXED + 1)) + origin
-                block = lowest >> 7
                 lower = jnp.floor(place)
                 fraction = place - lower
                 weight_low = (1.0 - fraction).astype(BF16).astype(F32)
                 weight_high = fraction.astype(BF16).astype(F32)
-                spot = lower.astype(jnp.int32) - block * LANES
+                spot = lower.astype(jnp.int32) - window * WINDOW
                 near = spot < LANES
                 inner = spot & (LANES - 1)
-                rows = slice(view * slices, (view + 1) * slices)
                 take = functools.partial(jnp.take_along_axis, indices=inner, axis=1, mode="promise_in_bounds")
-                low = jnp.where(near, take(low_ref[block, rows]), take(low_ref[block + 1, rows]))
-                high = jnp.where(near, take(high_ref[block, rows]), take(high_ref[block + 1, rows]))
+                low = jnp.where(near, take(low_near), take(low_far))
+                high = jnp.where(near, take(high_near), take(high_far))
                 totals[row] = totals[row] + (low * weight_low + high * weight_high)
         for row in range(ROW_DEV):
             part_ref[row * slices:(row + 1) * slices, pl.ds(pl.multiple_of(index * LANES, LANES), LANES)] = totals[row]
@@ -313,8 +322,8 @@
         out_specs=(vmem,) * 4,
         scratch_shapes=[
             pltpu.VMEM((bins // BLOCK * flat, BLOCK), F32),
-            pltpu.VMEM((extended // LANES, flat, LANES), F32),
-            pltpu.VMEM((extended // LANES, flat, LANES), F32),
+            pltpu.VMEM((extended // WINDOW, flat, LANES), F32),
+            pltpu.VMEM((extended // WINDOW, flat, LANES), F32),
             pltpu.VMEM((ROW_DEV * slices, bins // CHUNKS), F32),
             pltpu.VMEM((CHUNKS, slices, QUARTERS * ROW_DEV, span), BF16),
             pltpu.VMEM((slots, group_slices, QUARTERS * ROW_DEV, span), BF16),

time: 23.2 us -> 22.6 us (0.974)
  Pallas kernels: 23.1 us -> 22.5 us
    pallas_call x1, Pallas kernels: 20 us -> 19.4 us  [local(): pl.pallas_call(functools.partial(project_kernel, views, row_groups), out_...]
where the time goes in v3:
time: 22.6 us; the launch traced here: 22.5 us
  Pallas kernels  22.5 us (100%)
    pallas_call x1, Pallas kernels, local(): pl.pallas_call(functools.partial(project_kernel, views, row_groups), out_...  19.4 us
    pallas_call x1, Pallas kernels, local(): return conv(rows, one, two, second)  3.05 us

profile of v3, /device:TPU:1, one launch (start us, length us, event | category | flops | bytes accessed | tf_op | source)
XLA Modules:
  0.0 22.5 jit_solution(18089877846566432518)
XLA Ops:
  0.0 19.4 %project.1 = (f32[1,8,2048]{2,1,0:T(8,128)}, bf16[192,80]{1,0:T(8,128)(2,1)}, bf16[128,576]{1,0:T(8,128)(2,1)}, f32[128,128]{1,0:T(8,128)}) custom-call(bf16[8,8,2048]{2,1,0:T(8,128)(2,1)} %sino_ref.1, bf16[64,64]{1,0:T(8,128)(2,1)} %constant.18.clone.perm_in_ref, bf16[128,128]{1,0:T(8,128)(2,1)} %constant.19.clone.perm_out_ref, ...), custom_call_target="tpu_custom_call" | custom-call | tf_op jit(solution)/shard_map/project/pallas_call | solution.py:313
  19.4 3.1 %conv.1 = bf16[1,32,4,2048]{3,2,1,0:T(4,128)(2,1)} custom-call(f32[1,8,2048]{2,1,0:T(8,128)} %get-tuple-element.9.rows_ref, bf16[192,80]{1,0:T(8,128)(2,1)} %get-tuple-element.10.one_ref, bf16[128,576]{1,0:T(8,128)(2,1)} %get-tuple-element.11.two_ref, f32[128,128]{1,0:T(8,128)} %get-tuple-element.12.second_ref), custom_call_target="tpu_custom_call" | custom-call | tf_op jit(solution)/shard_map/conv/pallas_call | solution.py:351

commit v4 on v3

--- a/solution.py
+++ b/solution.py
@@ -14,7 +14,7 @@
 LANES = 128
 BLOCK = 256
 QUARTERS = 4
-CHUNKS = 2
+CHUNKS = 4
 FIXED = 18
 WINDOW = 64
 F32 = jnp.float32

time: 22.6 us -> 23.2 us (1.027)
  Pallas kernels: 22.5 us -> 23 us
    pallas_call x1, Pallas kernels: 19.4 us -> 20 us  [local(): pl.pallas_call(functools.partial(project_kernel, views, row_groups), out_...]
where the time goes in v4:
time: 23.2 us; the launch traced here: 23 us
  Pallas kernels  23 us (99%)
    pallas_call x1, Pallas kernels, local(): pl.pallas_call(functools.partial(project_kernel, views, row_groups), out_...  20 us
    pallas_call x1, Pallas kernels, local(): return conv(rows, one, two, second)  3.06 us

profile of v4, /device:TPU:1, one launch (start us, length us, event | category | flops | bytes accessed | tf_op | source)
XLA Modules:
  0.0 23.0 jit_solution(9357683461624857493)
XLA Ops:
  0.0 20.0 %project.1 = (f32[1,8,2048]{2,1,0:T(8,128)}, bf16[192,80]{1,0:T(8,128)(2,1)}, bf16[128,576]{1,0:T(8,128)(2,1)}, f32[128,128]{1,0:T(8,128)}) custom-call(bf16[8,8,2048]{2,1,0:T(8,128)(2,1)} %sino_ref.1, bf16[64,64]{1,0:T(8,128)(2,1)} %constant.18.clone.perm_in_ref, bf16[128,128]{1,0:T(8,128)(2,1)} %constant.19.clone.perm_out_ref, ...), custom_call_target="tpu_custom_call" | custom-call | tf_op jit(solution)/shard_map/project/pallas_call | solution.py:313
  20.0 3.1 %conv.1 = bf16[1,32,4,2048]{3,2,1,0:T(4,128)(2,1)} custom-call(f32[1,8,2048]{2,1,0:T(8,128)} %get-tuple-element.9.rows_ref, bf16[192,80]{1,0:T(8,128)(2,1)} %get-tuple-element.10.one_ref, bf16[128,576]{1,0:T(8,128)(2,1)} %get-tuple-element.11.two_ref, f32[128,128]{1,0:T(8,128)} %get-tuple-element.12.second_ref), custom_call_target="tpu_custom_call" | custom-call | tf_op jit(solution)/shard_map/conv/pallas_call | solution.py:351
